TPU v7x, 32 devices: a whole 2x2x4 slice. The times are simulated.
32 devices in a mesh: row: 8 (over y, x, core), col: 4 (over z).
Axes of the slice: x: 2, y: 2, z: 4, core: 2. Of those that a mesh axis runs over, the one named last changes fastest.
Arguments:
- tangents: float32 [192, 128, 6144], P('row', None, 'col'), may hold values from -6 to 6
- base_flow: float32 [192, 128, 192], P('row', None, 'col'), may hold values from -0.0625 to 0.0625
- mode_mask: int32 [192, 192], P('row', 'col'), may hold values 0 or 1
- decay_rates: float32 [128], replicated, may hold values from 1 to 100
- to_eigen: float32 [128, 128], replicated, may hold values from -0.5 to 0.5
- from_eigen: float32 [128, 128], replicated, may hold values from -0.5 to 0.5
Outputs:
- vectors: float32 [192, 128, 6144], P('row', None, 'col')
- growth: float32 [32], replicated
Inputs may be any that keep to these rules, and one draw needn't show every extreme that they name: `mode_mask`: 1 keeps a mode pair of the linearized product, 0 removes it.
All inputs are finite; a program needn't handle non-finite values. No bound on the sum of `mode_mask` on one device may be relied on, other than what follows from the above.
Results may differ from a plain program's by a relative error of at most 0.00005.
Values sent between devices are 32-bit elements; how exact they have to be, the bound alone decides.
A program may use at most 256 MiB of HBM per device.

v0:
```python
import functools

import jax
import jax.numpy as jnp
import numpy as np
from jax import lax
from jax.experimental import pallas as pl
from jax.experimental.pallas import tpu as pltpu
from jax.sharding import PartitionSpec as P

STEP_COEF = 10.0
VISCOSITY = 0.01
ALPHA_X = 0.5
BETA_Z = 1.0
LANES = 128
MESH = pl.DeviceIdType.MESH


def synthesis(points_count):
    points = np.arange(points_count)[:, None]
    mode_index = np.arange(points_count)[None, :]
    middle = points_count // 2
    wave_index = np.where(mode_index <= middle, mode_index, mode_index - middle)
    angles = (points * wave_index % points_count) * (2.0 * np.pi / points_count)
    return np.where(mode_index <= middle, np.cos(angles), np.sin(angles))


def analysis(points_count):
    mode_index = np.arange(points_count)
    middle = points_count // 2
    weights = np.where((mode_index == 0) | (mode_index == middle), 1.0, 2.0) / points_count
    return weights[:, None] * synthesis(points_count).T


def derivative_analysis(points_count, wave_scale):
    middle = points_count // 2
    derivative = np.zeros((points_count, points_count))
    inner = np.arange(1, middle)
    derivative[inner, middle + inner] = inner
    derivative[middle + inner, inner] = -inner
    return -wave_scale * (derivative @ analysis(points_count))


def split_parts(value):
    high = value.astype(jnp.bfloat16)
    low = (value - high.astype(jnp.float32)).astype(jnp.bfloat16)
    return high, low


def parts_dot(left, right, dims=(((1,), (0,)), ((), ()))):
    left_high, left_low = left
    right_high, right_low = right
    dot = lambda a, b: lax.dot_general(a, b, dims, preferred_element_type=jnp.float32)
    return dot(left_high, right_high) + (dot(left_high, right_low) + dot(left_low, right_high))


def wave_number(index, count):
    return jnp.where(index <= count // 2, index, index - count // 2).astype(jnp.float32)


def substep_kernel(
    row_devices, col_devices, vec_count, lane_parts, row_block,
    q_ref, base_ref, mask_ref, decay_ref, to_ref, from_ref, sx_ref, sp_ref, sz_ref, st_ref, az_ref, gx_ref,
    stepped_ref, gram_ref,
    fields, terms, spectrum, planes, blocks, speed, rows, keep, zwave, rates, old, high_ref, cross_ref, packed, slots,
    field_sem, field_sent, base_sem, base_sent, term_sem, term_sent, old_sem, out_sem, gram_sem, gram_sent,
    *halves
):
    all_devices = row_devices * col_devices
    x_length, y_count, zv_length = q_ref.shape
    part = zv_length // lane_parts
    plane_count = y_count // all_devices
    z_length = zv_length // vec_count
    x_count, z_count = x_length * row_devices, z_length * col_devices
    groups = x_length // row_block * lane_parts
    tiles = zv_length // LANES
    row, col = lax.axis_index("row"), lax.axis_index("col")
    me = row * col_devices + col

    def others(action):
        def visit(i, carry):
            device = lax.rem(me + i, all_devices)
            action(device, (lax.div(device, col_devices), lax.rem(device, col_devices)))
            return carry

        lax.fori_loop(1, all_devices, visit, 0)

    def send(source, target, sent, arrived, place):
        pltpu.make_async_remote_copy(
            src_ref=source, dst_ref=target, send_sem=sent, recv_sem=arrived, device_id=place, device_id_type=MESH
        ).start()

    def whole_wait(ref, semaphore):
        pltpu.make_async_copy(ref, ref, semaphore).wait()

    barrier = pltpu.get_barrier_semaphore()
    others(lambda device, place: pl.semaphore_signal(barrier, inc=1, device_id=place, device_id_type=MESH))
    pl.semaphore_wait(barrier, all_devices - 1)

    def send_fields(k, carry):
        target = fields.at[k, col, row]
        pltpu.make_async_copy(q_ref.at[:, me * plane_count + k, :], target, field_sem.at[k]).start()
        others(
            lambda device, place: send(
                q_ref.at[:, device * plane_count + k, :], target, field_sent, field_sem.at[k], place
            )
        )
        return carry

    send_fields(0, 0)
    spectrum[...] = base_ref[...].T

    def send_base(k, carry):
        target = planes.at[k, col * row_devices + row]
        pltpu.make_async_copy(spectrum.at[me * plane_count + k], target, base_sem).start()
        others(
            lambda device, place: send(
                spectrum.at[device * plane_count + k], target, base_sent, base_sem, place
            )
        )
        return carry

    lax.fori_loop(0, plane_count, send_base, 0)
    lax.fori_loop(1, plane_count, send_fields, 0)

    def place_of(g):
        block, lane_part = lax.div(g, lane_parts), lax.rem(g, lane_parts)
        lanes = pl.ds(pl.multiple_of(lane_part * part, LANES), part)
        some = pl.ds(pl.multiple_of(block * row_block, row_block), row_block)
        return lane_part, slice(None) if row_block == x_length else some, lanes

    def fetch(g):
        lane_part, some, lanes = place_of(g)
        slot = lax.rem(g, 2)
        return pltpu.make_async_copy(q_ref.at[some, :, lanes], old.at[slot], old_sem.at[slot])

    fetch(0).start()

    spread = (
        lax.broadcasted_iota(jnp.int32, (z_length, zv_length), 1) // vec_count
        == lax.broadcasted_iota(jnp.int32, (z_length, zv_length), 0)
    ).astype(jnp.bfloat16)
    kept = jnp.dot(mask_ref[...].astype(jnp.bfloat16), spread, preferred_element_type=jnp.float32)
    lane = lax.broadcasted_iota(jnp.int32, (1, zv_length), 1)
    waves = (BETA_Z * wave_number(col * z_length + lane // vec_count, z_count)) ** 2
    for p in range(lane_parts):
        keep[p] = kept[:, p * part : (p + 1) * part]
        zwave[p] = waves[:, p * part : (p + 1) * part]
    column = jnp.broadcast_to(decay_ref[...], (LANES, y_count)).T
    for t in range(part // LANES):
        rates[:, t * LANES : (t + 1) * LANES] = column
    if rows.shape[0] > x_count:
        rows[x_count:, :] = jnp.zeros((rows.shape[0] - x_count, LANES), jnp.float32)
    high_ref[...] = jnp.zeros_like(high_ref)
    cross_ref[...] = jnp.zeros_like(cross_ref)
    whole_wait(planes, base_sem)

    def plane(k, carry):
        for c in range(col_devices):
            for m in range(x_length):
                blocks[c, m * row_devices : (m + 1) * row_devices, :] = planes[
                    k, c * row_devices : (c + 1) * row_devices, m * z_length : (m + 1) * z_length
                ]
        partial = sum(
            parts_dot(
                split_parts(blocks[c]), split_parts(st_ref[c * z_length : (c + 1) * z_length, :])
            )
            for c in range(col_devices)
        )
        speed[...] = parts_dot(split_parts(partial), split_parts(sp_ref[...]), (((0,), (0,)), ((), ())))
        whole_wait(fields.at[k], field_sem.at[k])

        def gather(t, carry):
            c, lanes = lax.div(t, tiles), pl.ds(pl.multiple_of(lax.rem(t, tiles) * LANES, LANES), LANES)
            for r in range(row_devices):
                rows[r * x_length : (r + 1) * x_length, :] = fields[k, c, r, :, lanes]
            for h, half in enumerate(halves):
                half[pl.ds(pl.multiple_of(t * LANES, LANES), LANES), :] = rows[h * LANES : (h + 1) * LANES, :].T
            return carry

        lax.fori_loop(0, col_devices * tiles, gather, 0)
        sx = split_parts(sx_ref[...])
        sz = split_parts(sz_ref[...])
        az = split_parts(az_ref[...])
        gx = split_parts(gx_ref[...])

        def transform(pair, carry):
            for u in range(2):
                where = pl.ds(pair * 2 + u, z_count, stride=vec_count)
                field = jnp.concatenate([half[where, :] for half in halves], axis=1)
                field = parts_dot(split_parts(field), sx)
                field = parts_dot(sz, split_parts(field))
                field = field * speed[...]
                field = parts_dot(az, split_parts(field))
                field = parts_dot(split_parts(field), gx)
                for h, half in enumerate(halves):
                    half[where, :] = field[:, h * LANES : (h + 1) * LANES]
            return carry

        lax.fori_loop(0, vec_count // 2, transform, 0)

        def scatter(t, carry):
            c, lanes = lax.div(t, tiles), pl.ds(pl.multiple_of(lax.rem(t, tiles) * LANES, LANES), LANES)
            for h, half in enumerate(halves):
                known = min(x_count - h * LANES, LANES)
                flipped = half[pl.ds(pl.multiple_of(t * LANES, LANES), LANES), :].T
                rows[h * LANES : h * LANES + known, :] = flipped[:known]
            for r in range(row_devices):
                fields[k, c, r, :, lanes] = rows[r * x_length : (r + 1) * x_length, :]
            return carry

        lax.fori_loop(0, col_devices * tiles, scatter, 0)

        def send_terms(g, carry):
            lane_part, some, lanes = place_of(g)
            target = terms.at[lane_part, some, me * plane_count + k, :]
            pltpu.make_async_copy(fields.at[k, col, row, some, lanes], target, term_sem.at[g]).start()
            others(
                lambda device, place: send(
                    fields.at[k, place[1], place[0], some, lanes], target, term_sent, term_sem.at[g], place
                )
            )
            return carry

        lax.fori_loop(0, groups, send_terms, 0)
        return carry

    lax.fori_loop(0, plane_count, plane, 0)
    into, back = split_parts(to_ref[...]), split_parts(from_ref[...])
    batch = 2 if row_block % 2 == 0 else 1
    inner = lambda a, b: lax.dot_general(a, b, (((0,), (0,)), ((), ())), preferred_element_type=jnp.float32)

    def group(g, carry):
        lane_part, some, lanes = place_of(g)
        slot = lax.rem(g, 2)
        region = terms.at[lane_part, some]

        @pl.when(g + 1 < groups)
        def _():
            fetch(g + 1).start()

        fetch(g).wait()
        whole_wait(region, term_sem.at[g])
        first = lax.div(g, lane_parts) * row_block

        def advance(b, carry):
            highs, lows = [], []
            for u in range(batch):
                at = b * batch + u
                m = first + at
                right_side = STEP_COEF * old[slot, at] + terms[lane_part, m] * keep[lane_part, pl.ds(m, 1), :]
                wave_x = ALPHA_X * wave_number(row * x_length + m, x_count)
                wave_row = STEP_COEF + VISCOSITY * (wave_x * wave_x + zwave[lane_part])
                eigen_part = parts_dot(into, split_parts(right_side)) / (wave_row + rates[...])
                stepped = parts_dot(back, split_parts(eigen_part))
                terms[lane_part, m] = stepped
                high, low = split_parts(stepped)
                highs.append(high)
                lows.append(low)
            high, low = jnp.concatenate(highs, axis=0), jnp.concatenate(lows, axis=0)
            high_total, cross_total = high_ref[...], cross_ref[...]
            for t in range(part // LANES):
                tile = slice(t * LANES, (t + 1) * LANES)
                high_total += inner(high[:, tile], high[:, tile])
                cross_total += inner(high[:, tile], low[:, tile])
            high_ref[...] = high_total
            cross_ref[...] = cross_total
            return carry

        lax.fori_loop(0, row_block // batch, advance, 0)
        pltpu.make_async_copy(region, stepped_ref.at[some, :, lanes], out_sem).start()
        return carry

    lax.fori_loop(0, groups, group, 0)

    total = high_ref[...] + cross_ref[...] + cross_ref[...].T
    sides = LANES // vec_count
    lane = lax.broadcasted_iota(jnp.int32, (LANES, LANES), 1) // vec_count
    side = lax.broadcasted_iota(jnp.int32, (LANES, LANES), 0) // vec_count
    total = jnp.where(lane == side, total, 0.0)
    folded = sum(total[s * vec_count : (s + 1) * vec_count, :] for s in range(sides))
    folded = sum((pltpu.roll(folded, s * vec_count, 1) for s in range(1, sides)), folded)
    short = vec_count // sides
    packed[...] = sum(
        jnp.where(lane[:short] == s, folded[s * short : (s + 1) * short, :], 0.0) for s in range(sides)
    )
    slots[me] = packed[...]
    others(lambda device, place: send(packed, slots.at[me], gram_sent, gram_sem, place))
    arrived = slots.at[pl.ds(0, all_devices - 1)]
    whole_wait(arrived, gram_sem)
    gram_ref[...] = lax.fori_loop(
        0, all_devices, lambda i, value: value + slots[i], jnp.zeros(gram_ref.shape, jnp.float32)
    )
    whole_wait(arrived, gram_sent)
    whole_wait(terms, out_sem)
    for semaphore in (field_sent, term_sent):
        whole_wait(fields.at[:, pl.ds(0, col_devices - 1)], semaphore)
        whole_wait(fields.at[:, col_devices - 1, pl.ds(0, row_devices - 1)], semaphore)
    sent = y_count - plane_count
    whole_wait(spectrum.at[pl.ds(0, sent // 8 * 8)], base_sent)
    for _ in range(sent % 8):
        whole_wait(spectrum.at[0], base_sent)


def substep(tangents, base_flow, mode_mask, decay_rates, to_eigen, from_eigen, lane_parts):
    x_length, y_count, zv_length = tangents.shape
    z_length = base_flow.shape[2]
    vec_count = zv_length // z_length
    row_devices, col_devices = lax.axis_size("row"), lax.axis_size("col")
    all_devices = row_devices * col_devices
    x_count, z_count = x_length * row_devices, z_length * col_devices
    plane_count = y_count // all_devices
    part = zv_length // lane_parts
    row_block = 8 if x_length % 8 == 0 else x_length
    groups = x_length // row_block * lane_parts
    padded = -(-x_count // LANES) * LANES
    extra = padded - x_count
    table = lambda values: jnp.asarray(values.astype(np.float32))
    widen = lambda values: table(np.pad(values, ((0, extra), (0, extra))))
    sx = synthesis(x_count).T
    by_place = sx.reshape(row_devices, x_length, x_count).swapaxes(0, 1).reshape(x_count, x_count)
    tables = (
        widen(sx),
        table(np.pad(by_place, ((0, 0), (0, extra)))),
        table(synthesis(z_count)),
        table(synthesis(z_count).T),
        table(analysis(z_count)),
        widen(derivative_analysis(x_count, ALPHA_X).T),
    )
    base = jnp.transpose(base_flow, (0, 2, 1)).reshape(x_length * z_length, y_count)
    length = -(-base.shape[0] // LANES) * LANES
    base = jnp.pad(base, ((0, length - base.shape[0]), (0, 0)))
    here = pl.BlockSpec(memory_space=pltpu.VMEM)
    far = pl.BlockSpec(memory_space=pl.ANY)
    real = lambda *shape: pltpu.VMEM(shape, jnp.float32)
    dma = lambda *shape: pltpu.SemaphoreType.DMA(shape) if shape else pltpu.SemaphoreType.DMA
    short = vec_count * vec_count // LANES
    return pl.pallas_call(
        functools.partial(substep_kernel, row_devices, col_devices, vec_count, lane_parts, row_block),
        out_shape=(
            jax.ShapeDtypeStruct(tangents.shape, jnp.float32),
            jax.ShapeDtypeStruct((short, LANES), jnp.float32),
        ),
        in_specs=[far] + [here] * 11,
        out_specs=(far, here),
        scratch_shapes=[
            real(plane_count, col_devices, row_devices, x_length, zv_length),
            real(lane_parts, x_length, y_count, part),
            real(y_count, length),
            real(plane_count, all_devices, length),
            real(col_devices, x_count, z_length),
            real(z_count, padded),
            real(padded, LANES),
            real(lane_parts, x_length, part),
            real(lane_parts, 1, part),
            real(y_count, part),
            real(2, row_block, y_count, part),
            real(LANES, LANES),
            real(LANES, LANES),
            real(short, LANES),
            real(all_devices, short, LANES),
            dma(plane_count),
            dma(),
            dma(),
            dma(),
            dma(groups),
            dma(),
            dma(2),
            dma(),
            dma(),
            dma(),
        ]
        + [real(z_count * vec_count, LANES)] * (padded // LANES),
        compiler_params=pltpu.CompilerParams(
            collective_id=0, has_side_effects=True, vmem_limit_bytes=63 * 1024 * 1024
        ),
    )(tangents, base, mode_mask, decay_rates[None, :], to_eigen, from_eigen, *tables)


def combine_kernel(x_ref, w_ref, o_ref):
    weights = split_parts(w_ref[...])
    width = w_ref.shape[0]
    for g in range(x_ref.shape[2] // width):
        lanes = slice(g * width, (g + 1) * width)
        o_ref[0, :, lanes] = parts_dot(split_parts(x_ref[0, :, lanes]), weights)


def combine(stepped, weights):
    x_length, y_count, zv_length = stepped.shape
    one = pl.BlockSpec((1, y_count, zv_length), lambda m: (m, 0, 0))
    return pl.pallas_call(
        combine_kernel,
        grid=(x_length,),
        out_shape=jax.ShapeDtypeStruct(stepped.shape, jnp.float32),
        in_specs=[one, pl.BlockSpec(weights.shape, lambda m: (0, 0))],
        out_specs=one,
        compiler_params=pltpu.CompilerParams(vmem_limit_bytes=12 * 1024 * 1024),
    )(stepped, weights)


def body(tangents, base_flow, mode_mask, decay_rates, to_eigen, from_eigen):
    x_length, y_count, zv_length = tangents.shape
    z_length = base_flow.shape[2]
    vec_count = zv_length // z_length
    cells = x_length * lax.axis_size("row") * y_count * z_length * lax.axis_size("col")
    stepped, gram = substep(tangents, base_flow, mode_mask, decay_rates, to_eigen, from_eigen, 2)
    sides = LANES // vec_count
    gram_matrix = gram.reshape(vec_count // sides, sides, vec_count).swapaxes(0, 1)
    gram_matrix = gram_matrix.reshape(vec_count, vec_count) / cells
    lower_factor = jnp.linalg.cholesky(gram_matrix)
    identity = jnp.eye(vec_count, dtype=jnp.float32)
    inverse = jax.scipy.linalg.solve_triangular(lower_factor, identity, lower=True)
    width = 2 * LANES if zv_length % (2 * LANES) == 0 else LANES
    weights = jnp.kron(jnp.eye(width // vec_count, dtype=jnp.float32), inverse.T)
    return combine(stepped, weights), jnp.log(jnp.diagonal(lower_factor))


def solution(mesh):
    placed = (P("row", None, "col"), P("row", None, "col"), P("row", "col"), P(), P(), P())
    return jax.shard_map(
        body, mesh=mesh, in_specs=placed, out_specs=(P("row", None, "col"), P()), check_vma=False
    )
```

profile of v0, /device:TPU:0, one launch (start us, length us, event | category | flops | bytes accessed | tf_op | source)
XLA Modules:
  0.0 880.4 jit_solution(5620956601180621123)
XLA Ops:
  0.7 847.2 %shard_map.131 = (f32[24,128,1536]{2,1,0:T(8,128)}, f32[8,128]{1,0:T(8,128)}) custom-call(f32[24,128,1536]{2,1,0:T(8,128)} %q_ref.1, f32[1152,128]{1,0:T(8,128)} %bitcast.24, s32[24,48]{1,0:T(8,128)} %mask_ref.1, f32[1,128]{1,0:T(1,128)} %bitcast.26, f32[128,128]{1,0:T(8,128)} %to_ref.1, f32[128,128]{1,0:T(8,128)} %from_ref.1, ...), custom_call_target="tpu_custom_call" | custom-call | tf_op jit(solution)/shard_map/pallas_call | solution.py:338
  847.8 0.7 broadcast_multiply_fusion.1
  848.5 0.1 div.22
  848.6 0.1 copy.17
  848.7 2.9 cholesky.14
  851.6 0.6 compare_reduce_fusion
  852.3 0.7 select_bitcast_fusion
  852.9 2.4 custom-call.7
  855.4 0.2 fusion
  855.6 0.7 gather_fusion
  856.3 0.5 log.3
  856.8 0.1 broadcast_multiply_fusion
  857.0 0.3 mul.27.w_ref
  857.3 0.0 copy-start
  857.3 6.4 copy-done
  863.7 16.7 %shard_map.132 = f32[24,128,1536]{2,1,0:T(8,128)} custom-call(f32[24,128,1536]{2,1,0:T(8,128)S(1)} %copy-done, f32[256,256]{1,0:T(8,128)S(1)} %mul.27.w_ref), custom_call_target="tpu_custom_call" | custom-call | tf_op jit(solution)/shard_map/pallas_call | solution.py:391
  (5 shorter events, 0.1 us)
Async XLA Ops:
  857.3 6.4 copy-start
where the time goes:
time: 881 us; the launch traced here: 880 us
  Pallas kernels  864 us (98%)
    pallas_call x1, Pallas kernels, substep(): pl.pallas_call(functools.partial(substep_kernel, row_devices, col_devices...  847 us

commit v1 on v0

--- a/solution.py
+++ b/solution.py
@@ -54,6 +54,17 @@
     return dot(left_high, right_high) + (dot(left_high, right_low) + dot(left_low, right_high))
 
 
+def stacked(left):
+    high, low = split_parts(left)
+    top = jnp.concatenate([high, high], axis=1)
+    return jnp.concatenate([top, jnp.concatenate([low, jnp.zeros_like(low)], axis=1)], axis=0)
+
+
+def stacked_dot(left, right):
+    both = jnp.dot(left, jnp.concatenate(split_parts(right), axis=0), preferred_element_type=jnp.float32)
+    return both[: left.shape[0] // 2] + both[left.shape[0] // 2 :]
+
+
 def wave_number(index, count):
     return jnp.where(index <= count // 2, index, index - count // 2).astype(jnp.float32)
 
@@ -61,9 +72,9 @@
 def substep_kernel(
     row_devices, col_devices, vec_count, lane_parts, row_block,
     q_ref, base_ref, mask_ref, decay_ref, to_ref, from_ref, sx_ref, sp_ref, sz_ref, st_ref, az_ref, gx_ref,
-    stepped_ref, gram_ref,
-    fields, terms, spectrum, planes, blocks, speed, rows, keep, zwave, rates, old, high_ref, cross_ref, packed, slots,
-    field_sem, field_sent, base_sem, base_sent, term_sem, term_sent, old_sem, out_sem, gram_sem, gram_sent,
+    terms, gram_ref,
+    fields, spectrum, planes, blocks, speed, rows, keep, zwave, rates, old, both_ref, packed, slots,
+    field_sem, field_sent, base_sem, base_sent, term_sem, term_sent, old_sem, gram_sem, gram_sent,
     *halves
 ):
     all_devices = row_devices * col_devices
@@ -151,8 +162,7 @@
         rates[:, t * LANES : (t + 1) * LANES] = column
     if rows.shape[0] > x_count:
         rows[x_count:, :] = jnp.zeros((rows.shape[0] - x_count, LANES), jnp.float32)
-    high_ref[...] = jnp.zeros_like(high_ref)
-    cross_ref[...] = jnp.zeros_like(cross_ref)
+    both_ref[...] = jnp.zeros_like(both_ref)
     whole_wait(planes, base_sem)
 
     def plane(k, carry):
@@ -226,7 +236,7 @@
         return carry
 
     lax.fori_loop(0, plane_count, plane, 0)
-    into, back = split_parts(to_ref[...]), split_parts(from_ref[...])
+    into, back = stacked(to_ref[...]), stacked(from_ref[...])
     batch = 2 if row_block % 2 == 0 else 1
     inner = lambda a, b: lax.dot_general(a, b, (((0,), (0,)), ((), ())), preferred_element_type=jnp.float32)
 
@@ -251,29 +261,27 @@
                 right_side = STEP_COEF * old[slot, at] + terms[lane_part, m] * keep[lane_part, pl.ds(m, 1), :]
                 wave_x = ALPHA_X * wave_number(row * x_length + m, x_count)
                 wave_row = STEP_COEF + VISCOSITY * (wave_x * wave_x + zwave[lane_part])
-                eigen_part = parts_dot(into, split_parts(right_side)) / (wave_row + rates[...])
-                stepped = parts_dot(back, split_parts(eigen_part))
+                eigen_part = stacked_dot(into, right_side) / (wave_row + rates[...])
+                stepped = stacked_dot(back, eigen_part)
                 terms[lane_part, m] = stepped
                 high, low = split_parts(stepped)
                 highs.append(high)
                 lows.append(low)
             high, low = jnp.concatenate(highs, axis=0), jnp.concatenate(lows, axis=0)
-            high_total, cross_total = high_ref[...], cross_ref[...]
+            total = both_ref[...]
             for t in range(part // LANES):
                 tile = slice(t * LANES, (t + 1) * LANES)
-                high_total += inner(high[:, tile], high[:, tile])
-                cross_total += inner(high[:, tile], low[:, tile])
-            high_ref[...] = high_total
-            cross_ref[...] = cross_total
+                total += inner(high[:, tile], jnp.concatenate([high[:, tile], low[:, tile]], axis=1))
+            both_ref[...] = total
             return carry
 
         lax.fori_loop(0, row_block // batch, advance, 0)
-        pltpu.make_async_copy(region, stepped_ref.at[some, :, lanes], out_sem).start()
         return carry
 
     lax.fori_loop(0, groups, group, 0)
 
-    total = high_ref[...] + cross_ref[...] + cross_ref[...].T
+    cross = both_ref[:, LANES:]
+    total = both_ref[:, :LANES] + cross + cross.T
     sides = LANES // vec_count
     lane = lax.broadcasted_iota(jnp.int32, (LANES, LANES), 1) // vec_count
     side = lax.broadcasted_iota(jnp.int32, (LANES, LANES), 0) // vec_count
@@ -292,7 +300,6 @@
         0, all_devices, lambda i, value: value + slots[i], jnp.zeros(gram_ref.shape, jnp.float32)
     )
     whole_wait(arrived, gram_sent)
-    whole_wait(terms, out_sem)
     for semaphore in (field_sent, term_sent):
         whole_wait(fields.at[:, pl.ds(0, col_devices - 1)], semaphore)
         whole_wait(fields.at[:, col_devices - 1, pl.ds(0, row_devices - 1)], semaphore)
@@ -338,14 +345,13 @@
     return pl.pallas_call(
         functools.partial(substep_kernel, row_devices, col_devices, vec_count, lane_parts, row_block),
         out_shape=(
-            jax.ShapeDtypeStruct(tangents.shape, jnp.float32),
-            jax.ShapeDtypeStruct((short, LANES), jnp.float32),
+            pltpu.VMEM((lane_parts, x_length, y_count, part), jnp.float32),
+            pltpu.VMEM((short, LANES), jnp.float32),
         ),
-        in_specs=[far] + [here] * 11,
-        out_specs=(far, here),
+        in_specs=[pl.BlockSpec(memory_space=pltpu.HBM)] + [here] * 11,
+        out_specs=(here, here),
         scratch_shapes=[
             real(plane_count, col_devices, row_devices, x_length, zv_length),
-            real(lane_parts, x_length, y_count, part),
             real(y_count, length),
             real(plane_count, all_devices, length),
             real(col_devices, x_count, z_length),
@@ -355,8 +361,7 @@
             real(lane_parts, 1, part),
             real(y_count, part),
             real(2, row_block, y_count, part),
-            real(LANES, LANES),
-            real(LANES, LANES),
+            real(LANES, 2 * LANES),
             real(short, LANES),
             real(all_devices, short, LANES),
             dma(plane_count),
@@ -368,34 +373,91 @@
             dma(2),
             dma(),
             dma(),
-            dma(),
         ]
         + [real(z_count * vec_count, LANES)] * (padded // LANES),
         compiler_params=pltpu.CompilerParams(
-            collective_id=0, has_side_effects=True, vmem_limit_bytes=63 * 1024 * 1024
+            collective_id=0, has_side_effects=True, vmem_limit_bytes=42 * 1024 * 1024
         ),
     )(tangents, base, mode_mask, decay_rates[None, :], to_eigen, from_eigen, *tables)
 
 
-def combine_kernel(x_ref, w_ref, o_ref):
-    weights = split_parts(w_ref[...])
-    width = w_ref.shape[0]
-    for g in range(x_ref.shape[2] // width):
-        lanes = slice(g * width, (g + 1) * width)
-        o_ref[0, :, lanes] = parts_dot(split_parts(x_ref[0, :, lanes]), weights)
-
-
-def combine(stepped, weights):
-    x_length, y_count, zv_length = stepped.shape
-    one = pl.BlockSpec((1, y_count, zv_length), lambda m: (m, 0, 0))
+def combine_kernel(vec_count, cells, gram_ref, stepped_ref, out_ref, growth_ref, given, weights, give_sem):
+    lane_parts, x_length, y_count, part = stepped_ref.shape
+    slots = given.shape[0]
+    give = lambda i: pltpu.make_async_copy(given.at[lax.rem(i, slots)], out_ref.at[i], give_sem.at[lax.rem(i, slots)])
+    sides = LANES // vec_count
+    short = vec_count // sides
+    lane = lax.broadcasted_iota(jnp.int32, (vec_count, LANES), 1)
+    line = lax.broadcasted_iota(jnp.int32, (vec_count, LANES), 0)
+    gram = jnp.concatenate(
+        [gram_ref[...] if s == 0 else pltpu.roll(gram_ref[...], LANES - s * vec_count, 1) for s in range(sides)], axis=0
+    )
+    left = jnp.where(lane < vec_count, gram / cells, 0.0)
+    right = jnp.where(lane == line, 1.0, 0.0)
+    pivots = jnp.zeros((1, LANES), jnp.float32)
+    for j in range(vec_count):
+        column = jnp.broadcast_to(left[:, j : j + 1], (vec_count, LANES))
+        pivot = column[j : j + 1, :]
+        factor = jnp.where(line > j, column / pivot, 0.0)
+        pivots = jnp.where(lane[:1] == j, pivot, pivots)
+        left = left - factor * left[j : j + 1, :]
+        right = right - factor * right[j : j + 1, :]
+    roots = jnp.sqrt(pivots)
+    growth_ref[...] = jnp.log(roots)[:, :vec_count]
+    turned = jnp.concatenate([right] + [jnp.zeros((LANES - vec_count, LANES), jnp.float32)], axis=0).T
+    inverse = jnp.where(lane < vec_count, turned[:vec_count, :] / roots, 0.0)
+    spread = sum((pltpu.roll(inverse, s * vec_count, 1) for s in range(1, sides)), inverse)
+    spread = jnp.concatenate([spread] * sides, axis=0)
+    across = lax.broadcasted_iota(jnp.int32, (LANES, LANES), 1) // vec_count
+    down = lax.broadcasted_iota(jnp.int32, (LANES, LANES), 0) // vec_count
+    high, low = split_parts(jnp.where(across == down, spread, 0.0))
+    weights[...] = jnp.concatenate(
+        [jnp.concatenate([high, low], axis=1), jnp.concatenate([high, jnp.zeros_like(low)], axis=1)], axis=0
+    )
+
+    def mix(i, carry):
+        @pl.when(i >= slots)
+        def _():
+            give(i - slots).wait()
+
+        slot = lax.rem(i, slots)
+        for p in range(lane_parts):
+            lanes = [slice(t * LANES, (t + 1) * LANES) for t in range(part // LANES)]
+            whole = jnp.concatenate([stepped_ref[p, i, :, tile] for tile in lanes], axis=0)
+            mixed = jnp.dot(
+                jnp.concatenate(split_parts(whole), axis=1), weights[...], preferred_element_type=jnp.float32
+            )
+            mixed = mixed[:, :LANES] + mixed[:, LANES:]
+            for t in range(part // LANES):
+                first = p * part + t * LANES
+                given[slot, :, first : first + LANES] = mixed[t * y_count : (t + 1) * y_count]
+        give(i).start()
+        return carry
+
+    lax.fori_loop(0, x_length, mix, 0)
+    for i in range(max(x_length - slots, 0), x_length):
+        give(i).wait()
+
+
+def combine(stepped, gram, vec_count, cells):
+    lane_parts, x_length, y_count, part = stepped.shape
+    here = pl.BlockSpec(memory_space=pltpu.VMEM)
+    slots = min(6, x_length)
     return pl.pallas_call(
-        combine_kernel,
-        grid=(x_length,),
-        out_shape=jax.ShapeDtypeStruct(stepped.shape, jnp.float32),
-        in_specs=[one, pl.BlockSpec(weights.shape, lambda m: (0, 0))],
-        out_specs=one,
-        compiler_params=pltpu.CompilerParams(vmem_limit_bytes=12 * 1024 * 1024),
-    )(stepped, weights)
+        functools.partial(combine_kernel, vec_count, float(cells)),
+        out_shape=(
+            jax.ShapeDtypeStruct((x_length, y_count, lane_parts * part), jnp.float32),
+            jax.ShapeDtypeStruct((1, vec_count), jnp.float32),
+        ),
+        in_specs=[here, here],
+        out_specs=(pl.BlockSpec(memory_space=pltpu.HBM), here),
+        scratch_shapes=[
+            pltpu.VMEM((slots, y_count, lane_parts * part), jnp.float32),
+            pltpu.VMEM((2 * LANES, 2 * LANES), jnp.bfloat16),
+            pltpu.SemaphoreType.DMA((slots,)),
+        ],
+        compiler_params=pltpu.CompilerParams(vmem_limit_bytes=16 * 1024 * 1024),
+    )(gram, stepped)
 
 
 def body(tangents, base_flow, mode_mask, decay_rates, to_eigen, from_eigen):
@@ -403,16 +465,10 @@
     z_length = base_flow.shape[2]
     vec_count = zv_length // z_length
     cells = x_length * lax.axis_size("row") * y_count * z_length * lax.axis_size("col")
-    stepped, gram = substep(tangents, base_flow, mode_mask, decay_rates, to_eigen, from_eigen, 2)
-    sides = LANES // vec_count
-    gram_matrix = gram.reshape(vec_count // sides, sides, vec_count).swapaxes(0, 1)
-    gram_matrix = gram_matrix.reshape(vec_count, vec_count) / cells
-    lower_factor = jnp.linalg.cholesky(gram_matrix)
-    identity = jnp.eye(vec_count, dtype=jnp.float32)
-    inverse = jax.scipy.linalg.solve_triangular(lower_factor, identity, lower=True)
-    width = 2 * LANES if zv_length % (2 * LANES) == 0 else LANES
-    weights = jnp.kron(jnp.eye(width // vec_count, dtype=jnp.float32), inverse.T)
-    return combine(stepped, weights), jnp.log(jnp.diagonal(lower_factor))
+    lane_parts = max(p for p in range(1, 5) if zv_length // LANES % p == 0)
+    stepped, gram = substep(tangents, base_flow, mode_mask, decay_rates, to_eigen, from_eigen, lane_parts)
+    vectors, growth = combine(stepped, gram, vec_count, cells)
+    return vectors, growth[0]
 
 
 def solution(mesh):

time: 881 us -> 860 us (0.976)
  no operation moved by 1% of the time
where the time goes in v1:
time: 860 us
  Pallas kernels  859 us (100%)
    pallas_call x1, Pallas kernels, substep(): pl.pallas_call(functools.partial(substep_kernel, row_devices, col_devices...  845 us

profile of v1, /device:TPU:0, one launch (start us, length us, event | category | flops | bytes accessed | tf_op | source)
XLA Modules:
  0.0 860.1 jit_solution(13299626069587323807)
XLA Ops:
  0.6 844.8 %shard_map.131 = (f32[4,24,128,384]{3,2,1,0:T(8,128)S(1)}, f32[8,128]{1,0:T(8,128)S(1)}) custom-call(f32[24,128,1536]{2,1,0:T(8,128)} %q_ref.1, f32[1152,128]{1,0:T(8,128)} %bitcast.5, s32[24,48]{1,0:T(8,128)} %mask_ref.1, f32[1,128]{1,0:T(1,128)} %bitcast.6, f32[128,128]{1,0:T(8,128)} %to_ref.1, f32[128,128]{1,0:T(8,128)} %from_ref.1, ...), custom_call_target="tpu_custom_call" | custom-call | tf_op jit(solution)/shard_map/pallas_call | solution.py:345
  845.5 14.6 %shard_map.132 = (f32[24,128,1536]{2,1,0:T(8,128)}, f32[1,32]{1,0:T(1,128)}) custom-call(f32[8,128]{1,0:T(8,128)S(1)} %get-tuple-element.6.gram_ref, f32[4,24,128,384]{3,2,1,0:T(8,128)S(1)} %get-tuple-element.7.stepped_ref), custom_call_target="tpu_custom_call" | custom-call | tf_op jit(solution)/shard_map/pallas_call | solution.py:446

commit v2 on v1

--- a/solution.py
+++ b/solution.py
@@ -71,10 +71,10 @@
 
 def substep_kernel(
     row_devices, col_devices, vec_count, lane_parts, row_block,
-    q_ref, base_ref, mask_ref, decay_ref, to_ref, from_ref, sx_ref, sp_ref, sz_ref, st_ref, az_ref, gx_ref,
+    q_ref, base_far, to_far, from_far, sx_far, sp_far, sz_far, st_far, az_far, gx_far, mask_ref, decay_ref,
     terms, gram_ref,
-    fields, spectrum, planes, blocks, speed, rows, keep, zwave, rates, old, both_ref, packed, slots,
-    field_sem, field_sent, base_sem, base_sent, term_sem, term_sent, old_sem, gram_sem, gram_sent,
+    base_ref, to_ref, from_ref, sx_ref, sp_ref, sz_ref, st_ref, az_ref, gx_ref, fields, spectrum, planes, blocks, speed, rows, keep, zwave, rates, old, both_ref, packed, slots,
+    field_sem, field_sent, base_sem, base_sent, term_sem, term_sent, old_sem, gram_sem, gram_sent, load_sem,
     *halves
 ):
     all_devices = row_devices * col_devices
@@ -104,6 +104,24 @@
     def whole_wait(ref, semaphore):
         pltpu.make_async_copy(ref, ref, semaphore).wait()
 
+    loads = [
+        pltpu.make_async_copy(source, target, load_sem.at[i])
+        for i, (source, target) in enumerate(
+            (
+                (base_far, base_ref),
+                (to_far, to_ref),
+                (from_far, from_ref),
+                (sx_far, sx_ref),
+                (sp_far, sp_ref),
+                (sz_far, sz_ref),
+                (st_far, st_ref),
+                (az_far, az_ref),
+                (gx_far, gx_ref),
+            )
+        )
+    ]
+    for load in loads:
+        load.start()
     barrier = pltpu.get_barrier_semaphore()
     others(lambda device, place: pl.semaphore_signal(barrier, inc=1, device_id=place, device_id_type=MESH))
     pl.semaphore_wait(barrier, all_devices - 1)
@@ -119,6 +137,8 @@
         return carry
 
     send_fields(0, 0)
+    for load in loads:
+        load.wait()
     spectrum[...] = base_ref[...].T
 
     def send_base(k, carry):
@@ -338,7 +358,8 @@
     length = -(-base.shape[0] // LANES) * LANES
     base = jnp.pad(base, ((0, length - base.shape[0]), (0, 0)))
     here = pl.BlockSpec(memory_space=pltpu.VMEM)
-    far = pl.BlockSpec(memory_space=pl.ANY)
+    far = pl.BlockSpec(memory_space=pltpu.HBM)
+    loaded = (base, to_eigen, from_eigen) + tables
     real = lambda *shape: pltpu.VMEM(shape, jnp.float32)
     dma = lambda *shape: pltpu.SemaphoreType.DMA(shape) if shape else pltpu.SemaphoreType.DMA
     short = vec_count * vec_count // LANES
@@ -348,9 +369,10 @@
             pltpu.VMEM((lane_parts, x_length, y_count, part), jnp.float32),
             pltpu.VMEM((short, LANES), jnp.float32),
         ),
-        in_specs=[pl.BlockSpec(memory_space=pltpu.HBM)] + [here] * 11,
+        in_specs=[far] * (1 + len(loaded)) + [here] * 2,
         out_specs=(here, here),
-        scratch_shapes=[
+        scratch_shapes=[real(*value.shape) for value in loaded]
+        + [
             real(plane_count, col_devices, row_devices, x_length, zv_length),
             real(y_count, length),
             real(plane_count, all_devices, length),
@@ -373,18 +395,20 @@
             dma(2),
             dma(),
             dma(),
+            dma(len(loaded)),
         ]
         + [real(z_count * vec_count, LANES)] * (padded // LANES),
         compiler_params=pltpu.CompilerParams(
             collective_id=0, has_side_effects=True, vmem_limit_bytes=42 * 1024 * 1024
         ),
-    )(tangents, base, mode_mask, decay_rates[None, :], to_eigen, from_eigen, *tables)
+    )(tangents, *loaded, mode_mask, decay_rates[None, :])
 
 
 def combine_kernel(vec_count, cells, gram_ref, stepped_ref, out_ref, growth_ref, given, weights, give_sem):
     lane_parts, x_length, y_count, part = stepped_ref.shape
-    slots = given.shape[0]
-    give = lambda i: pltpu.make_async_copy(given.at[lax.rem(i, slots)], out_ref.at[i], give_sem.at[lax.rem(i, slots)])
+    slots, depth = given.shape[:2]
+    some = lambda i: pl.ds(i * depth, depth)
+    give = lambda i: pltpu.make_async_copy(given.at[lax.rem(i, slots)], out_ref.at[some(i)], give_sem.at[lax.rem(i, slots)])
     sides = LANES // vec_count
     short = vec_count // sides
     lane = lax.broadcasted_iota(jnp.int32, (vec_count, LANES), 1)
@@ -395,13 +419,18 @@
     left = jnp.where(lane < vec_count, gram / cells, 0.0)
     right = jnp.where(lane == line, 1.0, 0.0)
     pivots = jnp.zeros((1, LANES), jnp.float32)
-    for j in range(vec_count):
-        column = jnp.broadcast_to(left[:, j : j + 1], (vec_count, LANES))
-        pivot = column[j : j + 1, :]
-        factor = jnp.where(line > j, column / pivot, 0.0)
-        pivots = jnp.where(lane[:1] == j, pivot, pivots)
-        left = left - factor * left[j : j + 1, :]
-        right = right - factor * right[j : j + 1, :]
+    block = 8
+    for first in range(0, vec_count, block):
+        columns = [jnp.broadcast_to(left[:, first + a : first + a + 1], (vec_count, LANES)) for a in range(block)]
+        for a in range(block):
+            j = first + a
+            pivot = columns[a][j : j + 1, :]
+            factor = jnp.where(line > j, columns[a] * (1.0 / pivot), 0.0)
+            pivots = jnp.where(lane[:1] == j, pivot, pivots)
+            for b in range(a + 1, block):
+                columns[b] = columns[b] - factor * columns[b][j : j + 1, :]
+            left = left - factor * left[j : j + 1, :]
+            right = right - factor * right[j : j + 1, :]
     roots = jnp.sqrt(pivots)
     growth_ref[...] = jnp.log(roots)[:, :vec_count]
     turned = jnp.concatenate([right] + [jnp.zeros((LANES - vec_count, LANES), jnp.float32)], axis=0).T
@@ -421,28 +450,30 @@
             give(i - slots).wait()
 
         slot = lax.rem(i, slots)
-        for p in range(lane_parts):
-            lanes = [slice(t * LANES, (t + 1) * LANES) for t in range(part // LANES)]
-            whole = jnp.concatenate([stepped_ref[p, i, :, tile] for tile in lanes], axis=0)
+        tiles = [(p, slice(t * LANES, (t + 1) * LANES)) for p in range(lane_parts) for t in range(part // LANES)]
+        for b in range(depth):
+            m = i * depth + b
+            whole = jnp.concatenate([stepped_ref[p, m, :, tile] for p, tile in tiles], axis=0)
             mixed = jnp.dot(
                 jnp.concatenate(split_parts(whole), axis=1), weights[...], preferred_element_type=jnp.float32
             )
             mixed = mixed[:, :LANES] + mixed[:, LANES:]
-            for t in range(part // LANES):
-                first = p * part + t * LANES
-                given[slot, :, first : first + LANES] = mixed[t * y_count : (t + 1) * y_count]
+            for t in range(len(tiles)):
+                given[slot, b, :, t * LANES : (t + 1) * LANES] = mixed[t * y_count : (t + 1) * y_count]
         give(i).start()
         return carry
 
-    lax.fori_loop(0, x_length, mix, 0)
-    for i in range(max(x_length - slots, 0), x_length):
+    blocks = x_length // depth
+    lax.fori_loop(0, blocks, mix, 0)
+    for i in range(max(blocks - slots, 0), blocks):
         give(i).wait()
 
 
 def combine(stepped, gram, vec_count, cells):
     lane_parts, x_length, y_count, part = stepped.shape
     here = pl.BlockSpec(memory_space=pltpu.VMEM)
-    slots = min(6, x_length)
+    depth = 4 if x_length % 4 == 0 else 1
+    slots = min(4, x_length // depth)
     return pl.pallas_call(
         functools.partial(combine_kernel, vec_count, float(cells)),
         out_shape=(
@@ -452,7 +483,7 @@
         in_specs=[here, here],
         out_specs=(pl.BlockSpec(memory_space=pltpu.HBM), here),
         scratch_shapes=[
-            pltpu.VMEM((slots, y_count, lane_parts * part), jnp.float32),
+            pltpu.VMEM((slots, depth, y_count, lane_parts * part), jnp.float32),
             pltpu.VMEM((2 * LANES, 2 * LANES), jnp.bfloat16),
             pltpu.SemaphoreType.DMA((slots,)),
         ],

time: 860 us -> 854 us (level)
  no operation moved by 1% of the time
where the time goes in v2:
time: 854 us
  Pallas kernels  853 us (100%)
    pallas_call x1, Pallas kernels, substep(): pl.pallas_call(functools.partial(substep_kernel, row_devices, col_devices...  844 us

profile of v2, /device:TPU:0, one launch (start us, length us, event | category | flops | bytes accessed | tf_op | source)
XLA Modules:
  0.0 853.9 jit_solution(11953064184900620231)
XLA Ops:
  0.6 844.2 %shard_map.131 = (f32[4,24,128,384]{3,2,1,0:T(8,128)S(1)}, f32[8,128]{1,0:T(8,128)S(1)}) custom-call(f32[24,128,1536]{2,1,0:T(8,128)} %q_ref.1, f32[1152,128]{1,0:T(8,128)} %bitcast.5, f32[128,128]{1,0:T(8,128)} %to_far.1, f32[128,128]{1,0:T(8,128)} %from_far.1, f32[256,256]{1,0:T(8,128)} %constant.6.clone.sx_far, f32[192,256]{1,0:T(8,128)} %constant.14.clone.sp_far, ...), custom_call_target="tpu_custom_call" | custom-call | tf_op jit(solution)/shard_map/pallas_call | solution.py:366
  844.8 9.1 %shard_map.132 = (f32[24,128,1536]{2,1,0:T(8,128)}, f32[1,32]{1,0:T(1,128)}) custom-call(f32[8,128]{1,0:T(8,128)S(1)} %get-tuple-element.6.gram_ref, f32[4,24,128,384]{3,2,1,0:T(8,128)S(1)} %get-tuple-element.7.stepped_ref), custom_call_target="tpu_custom_call" | custom-call | tf_op jit(solution)/shard_map/pallas_call | solution.py:477

commit v3 on v2

--- a/solution.py
+++ b/solution.py
@@ -257,7 +257,7 @@
 
     lax.fori_loop(0, plane_count, plane, 0)
     into, back = stacked(to_ref[...]), stacked(from_ref[...])
-    batch = 2 if row_block % 2 == 0 else 1
+    batch = 4 if row_block % 4 == 0 else 1
     inner = lambda a, b: lax.dot_general(a, b, (((0,), (0,)), ((), ())), preferred_element_type=jnp.float32)
 
     def group(g, carry):
@@ -496,7 +496,7 @@
     z_length = base_flow.shape[2]
     vec_count = zv_length // z_length
     cells = x_length * lax.axis_size("row") * y_count * z_length * lax.axis_size("col")
-    lane_parts = max(p for p in range(1, 5) if zv_length // LANES % p == 0)
+    lane_parts = max(p for p in range(1, 7) if zv_length // LANES % p == 0)
     stepped, gram = substep(tangents, base_flow, mode_mask, decay_rates, to_eigen, from_eigen, lane_parts)
     vectors, growth = combine(stepped, gram, vec_count, cells)
     return vectors, growth[0]

time: 854 us -> 852 us (level)
  no operation moved by 1% of the time
where the time goes in v3:
time: 852 us
  Pallas kernels  851 us (100%)
    pallas_call x1, Pallas kernels, substep(): pl.pallas_call(functools.partial(substep_kernel, row_devices, col_devices...  842 us

profile of v3, /device:TPU:0, one launch (start us, length us, event | category | flops | bytes accessed | tf_op | source)
XLA Modules:
  0.0 851.7 jit_solution(12976091854020478275)
XLA Ops:
  0.6 842.0 %shard_map.131 = (f32[6,24,128,256]{3,2,1,0:T(8,128)S(1)}, f32[8,128]{1,0:T(8,128)S(1)}) custom-call(f32[24,128,1536]{2,1,0:T(8,128)} %q_ref.1, f32[1152,128]{1,0:T(8,128)} %bitcast.5, f32[128,128]{1,0:T(8,128)} %to_far.1, f32[128,128]{1,0:T(8,128)} %from_far.1, f32[256,256]{1,0:T(8,128)} %constant.6.clone.sx_far, f32[192,256]{1,0:T(8,128)} %constant.14.clone.sp_far, ...), custom_call_target="tpu_custom_call" | custom-call | tf_op jit(solution)/shard_map/pallas_call | solution.py:366
  842.7 9.1 %shard_map.132 = (f32[24,128,1536]{2,1,0:T(8,128)}, f32[1,32]{1,0:T(1,128)}) custom-call(f32[8,128]{1,0:T(8,128)S(1)} %get-tuple-element.6.gram_ref, f32[6,24,128,256]{3,2,1,0:T(8,128)S(1)} %get-tuple-element.7.stepped_ref), custom_call_target="tpu_custom_call" | custom-call | tf_op jit(solution)/shard_map/pallas_call | solution.py:477
